TPU v7x, 8 devices: a whole 2x2x1 slice. The times are simulated.
8 devices in a mesh: dp: 1 (over z), sp: 2 (over y), cp: 4 (over x, core).
Axes of the slice: x: 2, y: 2, z: 1, core: 2. Of those that a mesh axis runs over, the one named last changes fastest.
Arguments:
- hidden: bfloat16 [8, 2048, 4096], P('dp', ('cp', 'sp'))
- w_qkv: bfloat16 [4096, 3, 32, 128], replicated
- w_out: bfloat16 [32, 128, 4096], replicated
- norm_gain: bfloat16 [4096], replicated
- w_up: bfloat16 [4096, 16384], replicated
- b_up: bfloat16 [16384], replicated
- w_down: bfloat16 [16384, 4096], replicated
- b_down: bfloat16 [4096], replicated
Outputs:
- output: bfloat16 [8, 2048, 4096], P('dp', ('cp', 'sp'))
All inputs are finite; a program needn't handle non-finite values.
Results may differ from a plain program's by a relative error of at most 0.0103326.
Values are sent between devices in bfloat16 or wider.
A program may use at most 1.75 GiB of HBM per device.

v0:
```python
import functools
import math

import jax
import jax.numpy as jnp
from jax import lax
from jax.experimental import pallas as pl
from jax.experimental.pallas import tpu as pltpu
from jax.sharding import PartitionSpec as P

NORM_EPS = 1e-6
VMEM_BYTES = 63 * 2**20
BF = jnp.bfloat16
F32 = jnp.float32
ANY = pl.BlockSpec(memory_space=pl.ANY)

ORDER = (0, 2, 4, 1, 6, 3, 5, 7)
PIECES = 8


def peer(rel):
    i, j = lax.axis_index("cp"), lax.axis_index("sp")
    kx, kc, ky = rel // 4, (rel // 2) % 2, rel % 2
    x = lax.rem(i // 2 + kx, 2)
    core = lax.rem(lax.rem(i, 2) + kc, 2)
    cp, sp = x * 2 + core, lax.rem(j + ky, 2)
    return {"cp": cp, "sp": sp}, cp * 2 + sp


def arrive():
    bar = pltpu.get_barrier_semaphore()
    for rel in range(1, PIECES):
        pl.semaphore_signal(bar, inc=1, device_id=peer(rel)[0], device_id_type=pl.DeviceIdType.MESH)


def await_all():
    pl.semaphore_wait(pltpu.get_barrier_semaphore(), PIECES - 1)


def params(**kw):
    return pltpu.CompilerParams(vmem_limit_bytes=VMEM_BYTES, **kw)


def qkv_kernel(hid, w_hbm, o_ref, row_out, xs, wbuf, w_sem, own_sem, send_sem, recv_sem, out_sem, *, n_tiles, kp, group):
    t = pl.program_id(0)
    last = pl.num_programs(0) - 1
    chunk = t // n_tiles
    dim, hb, hd = wbuf.shape[1:]
    per = n_tiles // w_hbm.shape[1]

    def weights(step):
        tile = lax.rem(step, n_tiles)
        heads = pl.ds(pl.multiple_of(lax.rem(tile, per) * hb, hb), hb)
        return pltpu.make_async_copy(w_hbm.at[:, tile // per, heads], wbuf.at[lax.rem(step, 2)], w_sem.at[lax.rem(step, 2)])

    def send(slot):
        dev, row = peer(ORDER[slot])
        return pltpu.make_async_remote_copy(
            src_ref=hid.at[row], dst_ref=xs.at[slot], send_sem=send_sem.at[slot - 1], recv_sem=recv_sem.at[slot - 1],
            device_id=dev, device_id_type=pl.DeviceIdType.MESH)

    def keep(slot):
        return pltpu.make_async_copy(xs.at[slot], row_out.at[slot], out_sem.at[slot])

    @pl.when(t == 0)
    def _():
        own = pltpu.make_async_copy(hid.at[peer(0)[1]], xs.at[0], own_sem)
        own.start()
        weights(t).start()
        arrive()
        await_all()
        for slot in range(1, PIECES):
            send(slot).start()
        own.wait()
        keep(0).start()

    for c in range(PIECES // 2):
        @pl.when(t == c * n_tiles)
        def _(c=c):
            for slot in (2 * c, 2 * c + 1):
                if slot:
                    send(slot).wait_recv()
                    keep(slot).start()

    @pl.when(t < last)
    def _():
        weights(t + 1).start()

    weights(t).wait()

    w_ref = wbuf.at[lax.rem(t, 2)]
    for h in range(0, hb, group):
        acc = None
        for k in range(0, dim, kp):
            turned = jnp.swapaxes(w_ref[k:k + kp, h:h + group], 0, 1)
            cols = jnp.concatenate([turned[g] for g in range(group)], axis=1)
            x = xs[pl.ds(2 * chunk, 2), :, k:k + kp]
            d = jnp.dot(x.reshape(-1, kp), cols, preferred_element_type=F32)
            acc = d if acc is None else acc + d
        o_ref[:, h * hd:(h + group) * hd] = acc.astype(BF)

    @pl.when(t == last)
    def _():
        for slot in range(PIECES):
            if slot:
                send(slot).wait_send()
            keep(slot).wait()


def gather_qkv(hidden, w, hb=16):
    pieces, tok, dim = hidden.shape
    _, kinds, heads, head_dim = w.shape
    per, width, tn = heads // hb, kinds * heads * head_dim, hb * head_dim
    n_tiles = kinds * per
    return pl.pallas_call(
        functools.partial(qkv_kernel, n_tiles=n_tiles, kp=256, group=8), name="gather_qkv", grid=(pieces // 2 * n_tiles,),
        in_specs=[ANY, ANY],
        out_specs=[pl.BlockSpec((2 * tok, tn), lambda t: (t // n_tiles, t % n_tiles)), ANY],
        out_shape=[jax.ShapeDtypeStruct((pieces * tok, width), BF), jax.ShapeDtypeStruct(hidden.shape, BF)],
        scratch_shapes=[pltpu.VMEM(hidden.shape, BF), pltpu.VMEM((2, dim, hb, head_dim), BF), pltpu.SemaphoreType.DMA((2,)),
                        pltpu.SemaphoreType.DMA, pltpu.SemaphoreType.DMA((pieces - 1,)),
                        pltpu.SemaphoreType.DMA((pieces - 1,)), pltpu.SemaphoreType.DMA((pieces,))],
        compiler_params=params(collective_id=0, has_side_effects=True))(hidden, w)


def attn_kernel(q_ref, k_ref, v_ref, qn_ref, kn_ref, o_ref, ve_ref, sc_ref, *, bq, hd, dim):
    tok = q_ref.shape[0]
    n = tok // bq
    coef = dim ** -0.5 * math.log2(math.e)

    def dot_nt(a, b):
        return lax.dot_general(a, b, (((1,), (1,)), ((), ())), preferred_element_type=F32)

    @pl.when(pl.program_id(0) == 0)
    def _():
        ve_ref[:, dim:] = jnp.zeros((tok, dim), BF)
        sc_ref[...] = dot_nt(q_ref[:bq, :dim], k_ref[:, :dim])

    def scores(g):
        h, i = divmod(g, n)
        if h < hd:
            return dot_nt(q_ref[i * bq:(i + 1) * bq, h * dim:(h + 1) * dim], k_ref[:, h * dim:(h + 1) * dim])
        return dot_nt(qn_ref[...], kn_ref[...])

    s = sc_ref[...]
    for g in range(n * hd):
        h, i = divmod(g, n)
        if i == 0:
            ve_ref[:, :dim] = v_ref[:, h * dim:(h + 1) * dim]
        ahead = scores(g + 1)
        m = jnp.max(s, axis=-1, keepdims=True)
        p = jnp.exp2((s - m) * coef)
        total = jnp.sum(p, axis=-1, keepdims=True)
        o = jnp.dot(p.astype(BF), ve_ref[...], preferred_element_type=F32)
        o_ref[i * bq:(i + 1) * bq, h * dim:(h + 1) * dim] = (o[:, :dim] * (1.0 / total)).astype(BF)
        s = ahead
    sc_ref[...] = s


def attention(qkv, heads, dim, bq=256, hd=4):
    tok = qkv.shape[0]
    steps = heads // hd
    cols = lambda j: pl.BlockSpec((tok, hd * dim), lambda t: (0, j * steps + t))
    ahead = lambda t: jnp.minimum((t + 1) * hd, heads - 1)
    return pl.pallas_call(
        functools.partial(attn_kernel, bq=bq, hd=hd, dim=dim), name="attention", grid=(steps,),
        in_specs=[cols(0), cols(1), cols(2), pl.BlockSpec((bq, dim), lambda t: (0, ahead(t))),
                  pl.BlockSpec((tok, dim), lambda t: (0, heads + ahead(t)))],
        out_specs=pl.BlockSpec((tok, hd * dim), lambda t: (0, t)),
        out_shape=jax.ShapeDtypeStruct((tok, heads * dim), BF),
        scratch_shapes=[pltpu.VMEM((tok, 2 * dim), BF), pltpu.VMEM((bq, tok), F32)],
        compiler_params=params())(*[qkv] * 5)


TANH_LIN = math.sqrt(2 / math.pi)
TANH_CUB = TANH_LIN * 0.044715


def gelu(z):
    half = 0.5 * z
    return half + half * jnp.tanh(z * (TANH_LIN + TANH_CUB * (z * z)))


def up_kernel(r_hbm, v_ref, w_hbm, o_ref, xn, rbuf, z0, z1, wbuf, w_sem, sem, *, tm, tn, sub, kp, ep, rn):
    t = pl.program_id(0)
    tok, dim = xn.shape
    nm, last = tok // tm, pl.num_programs(0) - 1
    rc = rbuf.shape[1]

    def weights(n):
        cols = pl.ds(pl.multiple_of(n * tn, tn), tn)
        return pltpu.make_async_copy(w_hbm.at[:, cols], wbuf.at[lax.rem(n, 2)], w_sem.at[lax.rem(n, 2)])

    @pl.when(t == 0)
    def _():
        fetch = lambda i: pltpu.make_async_copy(r_hbm.at[pl.ds(i * rc, rc)], rbuf.at[lax.rem(i, 2)], sem.at[lax.rem(i, 2)])
        fetch(0).start()
        weights(0).start()
        gain = v_ref[:, :dim].astype(F32)

        def block(i, _):
            @pl.when(i + 1 < tok // rc)
            def _():
                fetch(i + 1).start()

            fetch(i).wait()

            def rows(u, _):
                at = pl.multiple_of(u * rn, rn)
                x = rbuf[lax.rem(i, 2), pl.ds(at, rn), :].astype(F32)
                inv = lax.rsqrt(jnp.mean(x * x, axis=-1, keepdims=True) + NORM_EPS)
                xn[pl.ds(pl.multiple_of(i * rc + at, rn), rn), :] = (x * inv * gain).astype(BF)
                return 0

            return lax.fori_loop(0, rc // rn, rows, 0)

        lax.fori_loop(0, tok // rc, block, 0)

    n = t // nm

    @pl.when((t < last) & (lax.rem(t, nm) == 0))
    def _():
        @pl.when(t + nm < last)
        def _():
            weights(n + 1).start()

        weights(n).wait()

    w_ref = wbuf.at[lax.rem(n, 2)]
    col = jnp.maximum((t - 1) // nm, 0) * tn
    bias = lambda: v_ref[:, pl.ds(pl.multiple_of(dim + col, tn), tn)].astype(F32)

    def tile(z_now, z_prev):
        base = pl.multiple_of(lax.rem(t, nm) * tm, tm)
        b = bias()
        parts = [(e, c) for e in range(0, tm, ep) for c in range(0, tn, sub)]
        share = len(parts) / (tm // sub * (tn // sub) * (dim // kp))
        done = step = 0
        for c in range(0, tn, sub):
            for r in range(0, tm, sub):
                acc = None
                for k in range(0, dim, kp):
                    d = jnp.dot(xn[pl.ds(base + r, sub), k:k + kp], w_ref[k:k + kp, c:c + sub], preferred_element_type=F32)
                    acc = d if acc is None else acc + d
                    step += 1
                    while done < step * share - 1e-9:
                        e, ec = parts[done]
                        done += 1
                        o_ref[e:e + ep, ec:ec + sub] = gelu(z_prev[e:e + ep, ec:ec + sub] + b[:, ec:ec + sub]).astype(BF)
                z_now[r:r + sub, c:c + sub] = acc

    for par, (za, zb) in enumerate(((z0, z1), (z1, z0))):
        @pl.when((t < last) & (lax.rem(t, 2) == par))
        def _(za=za, zb=zb):
            tile(za, zb)

    @pl.when(t == last)
    def _():
        o_ref[...] = gelu(z1[...] + bias()).astype(BF)


def norm_up(resid, vec, w, tm=1024, tn=1024):
    tok, dim = resid.shape
    nm = tok // tm
    tiles = nm * (w.shape[1] // tn)
    prev = lambda t: jnp.maximum(t - 1, 0)
    return pl.pallas_call(
        functools.partial(up_kernel, tm=tm, tn=tn, sub=512, kp=256, ep=32, rn=128), name="norm_up", grid=(tiles + 1,),
        in_specs=[ANY, pl.BlockSpec(vec.shape, lambda t: (0, 0)), ANY],
        out_specs=pl.BlockSpec((tm, tn), lambda t: (prev(t) % nm, prev(t) // nm)),
        out_shape=jax.ShapeDtypeStruct((tok, w.shape[1]), BF),
        scratch_shapes=[pltpu.VMEM((tok, dim), BF), pltpu.VMEM((2, 256, dim), BF), pltpu.VMEM((tm, tn), F32),
                        pltpu.VMEM((tm, tn), F32), pltpu.VMEM((2, dim, tn), BF), pltpu.SemaphoreType.DMA((2,)),
                        pltpu.SemaphoreType.DMA((2,))],
        compiler_params=params())(resid, vec, w)


SLOTS = 3


def down_kernel(a_ref, w_ref, r_ref, b_ref, out, acc, obuf, own_sem, send_sem, recv_sem, *, tn, nk, nn):
    t = pl.program_id(0)
    tiles = PIECES // 2 * nn
    q, k = t // nk, lax.rem(t, nk)
    tok = out.shape[1]

    def moves(tile):
        chunk = PIECES // 2 - 1 - tile // nn
        cols = pl.ds(tile % nn * tn, tn)
        my_row = peer(0)[1]
        for p in range(2):
            slot = 2 * chunk + p
            src = obuf.at[tile % SLOTS, pl.ds(p * tok, tok)]
            dst = out.at[my_row, :, cols]
            if slot == 0:
                yield pltpu.make_async_copy(src, dst, own_sem.at[tile % nn]), None
            else:
                yield None, pltpu.make_async_remote_copy(
                    src_ref=src, dst_ref=dst, send_sem=send_sem.at[tile, p], recv_sem=recv_sem.at[tile % nn, slot - 1],
                    device_id=peer(ORDER[slot])[0], device_id_type=pl.DeviceIdType.MESH)

    def sent(tile):
        for local, remote in moves(tile):
            if remote:
                remote.wait_send()
            else:
                local.wait()

    @pl.when(t == 0)
    def _():
        arrive()

    @pl.when(t == nk)
    def _():
        await_all()

    for tile in range(tiles):
        @pl.when(t == (tile + 1) * nk)
        def _(tile=tile):
            for local, remote in moves(tile):
                (local or remote).start()

        if tile + SLOTS < tiles:
            @pl.when(t == (tile + SLOTS) * nk + nk - 1)
            def _(tile=tile):
                sent(tile)

    @pl.when(q < tiles)
    def _():
        @pl.when(k < nk - 1)
        def _():
            d = jnp.dot(a_ref[...], w_ref[...], preferred_element_type=F32)
            acc[...] = jnp.where(k == 0, d, acc[...] + d)

        @pl.when(k == nk - 1)
        def _():
            d = jnp.dot(a_ref[...], w_ref[...], preferred_element_type=F32)
            y = r_ref[...].astype(F32) + ((acc[...] + d) + b_ref[...].astype(F32))
            obuf[lax.rem(q, SLOTS)] = y.astype(BF)

    @pl.when(q == tiles)
    def _():
        for tile in range(tiles - SLOTS, tiles):
            sent(tile)
        for tile in range(tiles):
            for _, remote in moves(tile):
                if remote:
                    remote.wait_recv()


def down_scatter(act, w, resid, b, tok, tn=2048, tk=4096):
    rows, kdim = act.shape
    dim = w.shape[1]
    tm, nn, nk = 2 * tok, dim // tn, kdim // tk
    tiles = PIECES // 2 * nn
    cur = lambda t: jnp.minimum(t, tiles * nk - 1)
    m_of = lambda t: PIECES // 2 - 1 - cur(t) // (nk * nn)
    n_of = lambda t: (cur(t) // nk) % nn
    return pl.pallas_call(
        functools.partial(down_kernel, tn=tn, nk=nk, nn=nn), name="down_scatter", grid=(tiles * nk + 1,),
        in_specs=[pl.BlockSpec((tm, tk), lambda t: (m_of(t), cur(t) % nk)),
                  pl.BlockSpec((tk, tn), lambda t: (cur(t) % nk, n_of(t))),
                  pl.BlockSpec((tm, tn), lambda t: (m_of(t), n_of(t))),
                  pl.BlockSpec((1, tn), lambda t: (0, b.shape[1] // tn - nn + n_of(t)))],
        out_specs=ANY, out_shape=jax.ShapeDtypeStruct((PIECES, tok, dim), BF),
        scratch_shapes=[pltpu.VMEM((tm, tn), F32), pltpu.VMEM((SLOTS, tm, tn), BF), pltpu.SemaphoreType.DMA((nn,)),
                        pltpu.SemaphoreType.DMA((tiles, 2)), pltpu.SemaphoreType.DMA((nn, PIECES - 1))],
        compiler_params=params(collective_id=1, has_side_effects=True))(act, w, resid, b)


def settle_kernel(x, out, buf, in_sem, out_sem):
    load = [pltpu.make_async_copy(x.at[i], buf.at[i], in_sem.at[i]) for i in range(PIECES)]
    save = [pltpu.make_async_copy(buf.at[i], out.at[i], out_sem.at[i]) for i in range(PIECES)]
    for c in load:
        c.start()
    for a, b in zip(load, save):
        a.wait()
        b.start()
    for c in save:
        c.wait()


def settle(x):
    return pl.pallas_call(
        settle_kernel, name="settle", in_specs=[ANY], out_specs=ANY, out_shape=jax.ShapeDtypeStruct(x.shape, x.dtype),
        scratch_shapes=[pltpu.VMEM(x.shape, x.dtype), pltpu.SemaphoreType.DMA((PIECES,)), pltpu.SemaphoreType.DMA((PIECES,))],
        compiler_params=params())(x)


def solution(mesh):
    tok_spec = P("dp", ("cp", "sp"), None)

    def local_block(hidden, w_qkv, w_out, norm_gain, w_up, b_up, w_down, b_down):
        pieces, tok, dim = hidden.shape
        _, _, heads, head_dim = w_qkv.shape
        qkv, row = gather_qkv(hidden, w_qkv)
        attn = attention(qkv, heads, head_dim)
        attn_out = jnp.dot(attn, w_out.reshape(heads * head_dim, dim), preferred_element_type=F32).astype(BF)
        resid = (row.reshape(pieces * tok, dim).astype(F32) + attn_out.astype(F32)).astype(BF)
        vec = jnp.concatenate([norm_gain, b_up, b_down]).reshape(1, -1)
        act = norm_up(resid, vec, w_up)
        return settle(down_scatter(act, w_down, resid, vec, tok))

    return jax.shard_map(local_block, mesh=mesh, in_specs=(tok_spec, P(), P(), P(), P(), P(), P(), P()), out_specs=tok_spec, check_vma=False)
```

profile of v0, /device:TPU:0, one launch (start us, length us, event | category | flops | bytes accessed | tf_op | source)
XLA Modules:
  0.0 1117.3 jit_solution(9007932722728645843)
XLA Ops:
  0.0 0.8 pad_maximum_fusion
  0.8 0.7 reshape.10.v_ref.b_ref
  1.5 240.6 %gather_qkv.1 = (bf16[2048,12288]{1,0:T(8,128)(2,1)}, bf16[8,256,4096]{2,1,0:T(8,128)(2,1)}) custom-call(bf16[8,256,4096]{2,1,0:T(8,128)(2,1)} %hid.1, bf16[4096,3,32,128]{3,2,1,0:T(8,128)(2,1)} %w_hbm.2), custom_call_target="tpu_custom_call" | custom-call | tf_op jit(solution)/shard_map/gather_qkv/pallas_call | solution.py:115
  242.1 178.3 %attention.1 = bf16[2048,4096]{1,0:T(8,128)(2,1)} custom-call(bf16[2048,12288]{1,0:T(8,128)(2,1)} %get-tuple-element.8.q_ref.k_ref.v_ref.qn_ref.kn_ref, bf16[2048,12288]{1,0:T(8,128)(2,1)} %get-tuple-element.8.q_ref.k_ref.v_ref.qn_ref.kn_ref, bf16[2048,12288]{1,0:T(8,128)(2,1)} %get-tuple-element.8.q_ref.k_ref.v_ref.qn_ref.kn_ref, ...), custom_call_target="tpu_custom_call" | custom-call | tf_op jit(solution)/shard_map/attention/pallas_call | solution.py:165
  420.4 80.3 %fusion.r_hbm.r_ref = bf16[2048,4096]{1,0:T(8,128)(2,1)} fusion(bf16[8,256,4096]{2,1,0:T(8,128)(2,1)} %get-tuple-element.7, bf16[2048,4096]{1,0:T(8,128)(2,1)} %attention.1, bf16[4096,4096]{1,0:T(8,128)(2,1)} %bitcast.6), kind=kOutput, calls=%fused_computation.1 | convolution fusion | flops 68761419776 | bytes 83886080 | tf_op jit(solution)/shard_map/dot_general | solution.py:398
  500.7 302.1 %norm_up.1.a_ref = bf16[2048,16384]{1,0:T(8,128)(2,1)} custom-call(bf16[2048,4096]{1,0:T(8,128)(2,1)} %fusion.r_hbm.r_ref, bf16[1,24576]{1,0:T(2,128)(2,1)} %reshape.10.v_ref.b_ref, bf16[4096,16384]{1,0:T(8,128)(2,1)} %w_hbm.3), custom_call_target="tpu_custom_call" | custom-call | tf_op jit(solution)/shard_map/norm_up/pallas_call | solution.py:267
  802.8 302.3 %down_scatter.1.x = bf16[8,256,4096]{2,1,0:T(8,128)(2,1)} custom-call(bf16[2048,16384]{1,0:T(8,128)(2,1)} %norm_up.1.a_ref, bf16[16384,4096]{1,0:T(8,128)(2,1)} %w_ref.1, bf16[2048,4096]{1,0:T(8,128)(2,1)} %fusion.r_hbm.r_ref, bf16[1,24576]{1,0:T(2,128)(2,1)} %reshape.10.v_ref.b_ref), custom_call_target="tpu_custom_call" | custom-call | tf_op jit(solution)/shard_map/down_scatter/pallas_call | solution.py:359
  1105.1 11.8 %settle.1 = bf16[8,256,4096]{2,1,0:T(8,128)(2,1)} custom-call(bf16[8,256,4096]{2,1,0:T(8,128)(2,1)} %down_scatter.1.x), custom_call_target="tpu_custom_call" | custom-call | tf_op jit(solution)/shard_map/settle/pallas_call | solution.py:384
where the time goes:
time: 1120 us
  Pallas kernels  1040 us (93%)
  matrix products  80.3 us (7%)
    pallas_call x1, Pallas kernels, down_scatter(): pl.pallas_call(functools.partial(down_kernel, tn=tn, nk=nk, nn=nn), name=...  302 us
    pallas_call x1, Pallas kernels, norm_up(): pl.pallas_call(functools.partial(up_kernel, tm=tm, tn=tn, sub=512, kp=256...  302 us
    pallas_call x1, Pallas kernels, gather_qkv(): pl.pallas_call(functools.partial(qkv_kernel, n_tiles=n_tiles, kp=256, gro...  241 us
    pallas_call x1, Pallas kernels, attention(): pl.pallas_call(functools.partial(attn_kernel, bq=bq, hd=hd, dim=dim), nam...  178 us
    dot_general x1, matrix products, local_block(): jnp.dot(attn, w_out.reshape(heads * head_dim, dim), preferred_element_typ...  80.3 us

commit v1 on v0

--- a/solution.py
+++ b/solution.py
@@ -256,7 +256,12 @@
 
     @pl.when(t == last)
     def _():
-        o_ref[...] = gelu(z1[...] + bias()).astype(BF)
+        def rows(i, _):
+            at = pl.ds(pl.multiple_of(i * 64, 64), 64)
+            o_ref[at, :] = gelu(z1[at, :] + bias()).astype(BF)
+            return 0
+
+        lax.fori_loop(0, tm // 64, rows, 0)
 
 
 def norm_up(resid, vec, w, tm=1024, tn=1024):

time: 1120 us -> 1110 us (level)
  Pallas kernels: 1040 us -> 1020 us
    pallas_call x1, Pallas kernels: 178 us -> 164 us  [attention(): pl.pallas_call(functools.partial(attn_kernel, bq=bq, hd=hd, dim=dim), nam...]
where the time goes in v1:
time: 1110 us; the launch traced here: 1100 us
  Pallas kernels  1020 us (92%)
  matrix products  80.3 us (7%)
    pallas_call x1, Pallas kernels, norm_up(): pl.pallas_call(functools.partial(up_kernel, tm=tm, tn=tn, sub=512, kp=256...  302 us
    pallas_call x1, Pallas kernels, down_scatter(): pl.pallas_call(functools.partial(down_kernel, tn=tn, nk=nk, nn=nn), name=...  302 us
    pallas_call x1, Pallas kernels, gather_qkv(): pl.pallas_call(functools.partial(qkv_kernel, n_tiles=n_tiles, kp=256, gro...  241 us
    pallas_call x1, Pallas kernels, attention(): pl.pallas_call(functools.partial(attn_kernel, bq=bq, hd=hd, dim=dim), nam...  164 us
    dot_general x1, matrix products, local_block(): jnp.dot(attn, w_out.reshape(heads * head_dim, dim), preferred_element_typ...  80.3 us

profile of v1, /device:TPU:0, one launch (start us, length us, event | category | flops | bytes accessed | tf_op | source)
XLA Modules:
  0.0 1103.3 jit_solution(6197014449415950886)
XLA Ops:
  0.0 0.8 pad_maximum_fusion
  0.8 0.7 reshape.10.v_ref.b_ref
  1.5 240.6 %gather_qkv.1 = (bf16[2048,12288]{1,0:T(8,128)(2,1)}, bf16[8,256,4096]{2,1,0:T(8,128)(2,1)}) custom-call(bf16[8,256,4096]{2,1,0:T(8,128)(2,1)} %hid.1, bf16[4096,3,32,128]{3,2,1,0:T(8,128)(2,1)} %w_hbm.2), custom_call_target="tpu_custom_call" | custom-call | tf_op jit(solution)/shard_map/gather_qkv/pallas_call | solution.py:115
  242.1 163.9 %attention.1 = bf16[2048,4096]{1,0:T(8,128)(2,1)} custom-call(bf16[2048,12288]{1,0:T(8,128)(2,1)} %get-tuple-element.8.q_ref.k_ref.v_ref.qn_ref.kn_ref, bf16[2048,12288]{1,0:T(8,128)(2,1)} %get-tuple-element.8.q_ref.k_ref.v_ref.qn_ref.kn_ref, bf16[2048,12288]{1,0:T(8,128)(2,1)} %get-tuple-element.8.q_ref.k_ref.v_ref.qn_ref.kn_ref, ...), custom_call_target="tpu_custom_call" | custom-call | tf_op jit(solution)/shard_map/attention/pallas_call | solution.py:165
  406.0 80.3 %fusion.r_hbm.r_ref = bf16[2048,4096]{1,0:T(8,128)(2,1)} fusion(bf16[8,256,4096]{2,1,0:T(8,128)(2,1)} %get-tuple-element.7, bf16[2048,4096]{1,0:T(8,128)(2,1)} %attention.1, bf16[4096,4096]{1,0:T(8,128)(2,1)} %bitcast.6), kind=kOutput, calls=%fused_computation.1 | convolution fusion | flops 68761419776 | bytes 83886080 | tf_op jit(solution)/shard_map/dot_general | solution.py:403
  486.4 302.4 %norm_up.1.a_ref = bf16[2048,16384]{1,0:T(8,128)(2,1)} custom-call(bf16[2048,4096]{1,0:T(8,128)(2,1)} %fusion.r_hbm.r_ref, bf16[1,24576]{1,0:T(2,128)(2,1)} %reshape.10.v_ref.b_ref, bf16[4096,16384]{1,0:T(8,128)(2,1)} %w_hbm.3), custom_call_target="tpu_custom_call" | custom-call | tf_op jit(solution)/shard_map/norm_up/pallas_call | solution.py:272
  788.7 302.3 %down_scatter.1.x = bf16[8,256,4096]{2,1,0:T(8,128)(2,1)} custom-call(bf16[2048,16384]{1,0:T(8,128)(2,1)} %norm_up.1.a_ref, bf16[16384,4096]{1,0:T(8,128)(2,1)} %w_ref.1, bf16[2048,4096]{1,0:T(8,128)(2,1)} %fusion.r_hbm.r_ref, bf16[1,24576]{1,0:T(2,128)(2,1)} %reshape.10.v_ref.b_ref), custom_call_target="tpu_custom_call" | custom-call | tf_op jit(solution)/shard_map/down_scatter/pallas_call | solution.py:364
  1091.0 11.8 %settle.1 = bf16[8,256,4096]{2,1,0:T(8,128)(2,1)} custom-call(bf16[8,256,4096]{2,1,0:T(8,128)(2,1)} %down_scatter.1.x), custom_call_target="tpu_custom_call" | custom-call | tf_op jit(solution)/shard_map/settle/pallas_call | solution.py:389
